TPU v7x, 32 devices: a 4x2x2 block of a 4x4x8 slice. The times are simulated.
32 devices in a mesh: dp: 4 (over y, z), tp: 8 (over x, core).
Axes of the slice: x: 4, y: 2, z: 2, core: 2. Of those that a mesh axis runs over, the one named last changes fastest.
The devices are a block of a 4x4x8 slice.
Arguments:
- tok_ids: int32 [16, 1536], P('dp'), parts along dimension 0
- pad_mask: int32 [16, 1536], P('dp'), parts along dimension 0
- emb_table: bfloat16 [250880, 2048], P('tp')
- ln_emb_w: bfloat16 [2048], replicated
- ln_emb_b: bfloat16 [2048], replicated
- ln1_w: bfloat16 [2048], replicated
- ln1_b: bfloat16 [2048], replicated
- w_qkv: bfloat16 [2048, 16, 3, 128], P(None, 'tp')
- b_qkv: bfloat16 [16, 3, 128], P('tp')
- w_out: bfloat16 [2048, 2048], P('tp')
- b_out: bfloat16 [2048], replicated
- ln2_w: bfloat16 [2048], replicated
- ln2_b: bfloat16 [2048], replicated
- w_up: bfloat16 [2048, 8192], P(None, 'tp')
- b_up: bfloat16 [8192], P('tp')
- w_down: bfloat16 [8192, 2048], P('tp')
- b_down: bfloat16 [2048], replicated
Outputs:
- output: bfloat16 [16, 1536, 2048], P('dp', 'tp'), parts along dimension 0
There are 4 independent parts. A program takes and returns all parts, laid end to end along the dimension named above; an argument that names none is the same for every part.
All inputs are finite; a program needn't handle non-finite values.
Results may differ from a plain program's by a relative error of at most 0.0139903.
Values are sent between devices in bfloat16 or wider.
A program may use at most 768 MiB of HBM per device.

v0:
```python
import math
import jax
import jax.numpy as jnp
from jax import lax
from jax.sharding import PartitionSpec as P

LN_EPS = 1e-5


def alibi_slopes(n_heads):
    closest = 2 ** int(math.floor(math.log2(n_heads)))
    base_ratio = 2.0 ** (-(2.0 ** -(math.log2(closest) - 3)))
    extra_ratio = 2.0 ** (-(2.0 ** -(math.log2(2 * closest) - 3)))
    first_part = [base_ratio ** step_k for step_k in range(1, closest + 1)]
    second_part = [extra_ratio ** step_k for step_k in range(1, 2 * (n_heads - closest), 2)]
    return first_part + second_part


def layer_norm(values_in, ln_gain, ln_shift):
    values_in = values_in.astype(jnp.float32)
    mean_v = jnp.mean(values_in, axis=-1, keepdims=True)
    centered = values_in - mean_v
    var_v = jnp.mean(centered * centered, axis=-1, keepdims=True)
    scaled = centered * lax.rsqrt(var_v + LN_EPS)
    return (scaled * ln_gain.astype(jnp.float32) + ln_shift.astype(jnp.float32)).astype(jnp.bfloat16)


def bloom_gelu(values_in):
    return values_in * 0.5 * (1.0 + jnp.tanh(0.79788456 * values_in * (1.0 + 0.044715 * values_in * values_in)))


def attention_block(normed_all, pad_mask, w_qkv, b_qkv, head_slopes):
    seq_len = normed_all.shape[1]
    head_dim = w_qkv.shape[3]
    qkv_all = (jnp.einsum('bsd,dhce->bshce', normed_all, w_qkv, preferred_element_type=jnp.float32) + b_qkv.astype(jnp.float32)).astype(jnp.bfloat16)
    queries = qkv_all[:, :, :, 0]
    key_vals = qkv_all[:, :, :, 1]
    values = qkv_all[:, :, :, 2]
    positions = jnp.arange(seq_len)
    distance = (positions[None, :] - positions[:, None]).astype(jnp.float32)
    causal = positions[None, :] <= positions[:, None]
    diagonal = positions[None, :] == positions[:, None]
    allowed = (causal[None] & (pad_mask[:, None, :] == 1)) | diagonal[None]
    scores = jnp.einsum('bqhd,bkhd->bhqk', queries, key_vals, preferred_element_type=jnp.float32) * (head_dim ** -0.5) + head_slopes[None, :, None, None] * distance[None, None]
    scores = jnp.where(allowed[:, None], scores, -1e30)
    attn_probs = jax.nn.softmax(scores, axis=-1).astype(jnp.bfloat16)
    context = jnp.einsum('bhqk,bkhd->bqhd', attn_probs, values, preferred_element_type=jnp.float32).astype(jnp.bfloat16)
    return context.reshape(context.shape[0], seq_len, -1)


def solution(mesh):
    n_tp = mesh.shape['tp']

    def local_step(tok_ids, pad_mask, emb_shard, ln_emb_w, ln_emb_b, ln1_w, ln1_b, w_qkv, b_qkv, w_out, b_out, ln2_w, ln2_b, w_up, b_up, w_down, b_down):
        tp_rank = lax.axis_index('tp')
        vocab_loc = emb_shard.shape[0]
        heads_loc = w_qkv.shape[1]
        local_ids = tok_ids - tp_rank * vocab_loc
        in_range = (local_ids >= 0) & (local_ids < vocab_loc)
        looked_up = jnp.take(emb_shard, jnp.clip(local_ids, 0, vocab_loc - 1), axis=0)
        partial_emb = jnp.where(in_range[:, :, None], looked_up, jnp.zeros((), jnp.bfloat16))
        embedded = lax.psum_scatter(partial_emb, 'tp', scatter_dimension=1, tiled=True)
        resid_in = layer_norm(embedded, ln_emb_w, ln_emb_b)
        normed = layer_norm(resid_in, ln1_w, ln1_b)
        normed_all = lax.all_gather(normed, 'tp', axis=1, tiled=True)
        all_slopes = jnp.array(alibi_slopes(heads_loc * n_tp), jnp.float32)
        head_slopes = lax.dynamic_slice_in_dim(all_slopes, tp_rank * heads_loc, heads_loc)
        context = attention_block(normed_all, pad_mask, w_qkv, b_qkv, head_slopes)
        attn_part = jnp.einsum('bsf,fd->bsd', context, w_out, preferred_element_type=jnp.float32).astype(jnp.bfloat16)
        attn_sum = lax.psum_scatter(attn_part, 'tp', scatter_dimension=1, tiled=True)
        resid_mid = (resid_in.astype(jnp.float32) + attn_sum.astype(jnp.float32) + b_out.astype(jnp.float32)).astype(jnp.bfloat16)
        normed2 = layer_norm(resid_mid, ln2_w, ln2_b)
        normed2_all = lax.all_gather(normed2, 'tp', axis=1, tiled=True)
        hidden_up = jnp.einsum('bsd,df->bsf', normed2_all, w_up, preferred_element_type=jnp.float32) + b_up.astype(jnp.float32)
        activated = bloom_gelu(hidden_up).astype(jnp.bfloat16)
        down_part = jnp.einsum('bsf,fd->bsd', activated, w_down, preferred_element_type=jnp.float32).astype(jnp.bfloat16)
        down_sum = lax.psum_scatter(down_part, 'tp', scatter_dimension=1, tiled=True)
        return (resid_mid.astype(jnp.float32) + down_sum.astype(jnp.float32) + b_down.astype(jnp.float32)).astype(jnp.bfloat16)

    replicated = P(None)
    in_specs = (P('dp', None), P('dp', None), P('tp', None), replicated, replicated, replicated, replicated, P(None, 'tp', None, None), P('tp', None, None), P('tp', None), replicated, replicated, replicated, P(None, 'tp'), P('tp'), P('tp', None), replicated)
    return jax.shard_map(local_step, mesh=mesh, in_specs=in_specs, out_specs=P('dp', 'tp', None), check_vma=False)
```

profile of v0, /device:TPU:81, one launch (start us, length us, event | category | flops | bytes accessed | tf_op | source)
XLA Modules:
  0.0 1208.2 jit_solution(17185306510033997452)
XLA Ops:
  6.5 0.0 copy-start
  6.6 0.0 reduce-scatter.4.cloned.1.call-start
  6.6 0.9 compare_and_fusion
  7.5 318.8 %gather_fusion = bf16[6144,2048]{1,0:T(8,128)(2,1)} fusion(bf16[31360,2048]{1,0:T(8,128)(2,1)} %param.20, s32[6144]{0:T(1024)S(1)} %broadcast_clamp_fusion), kind=kCustom, calls=%fused_computation | custom fusion | bytes 50356224 | tf_op jit(solution)/shard_map/jit(_take)/gather | solution.py:60
  326.2 21.4 %select_select_fusion = bf16[4,1536,2048]{2,1,0:T(8,128)(2,1)} fusion(bf16[4,1536,2048]{2,1,0:T(8,128)(2,1)} %bitcast.54, pred[4,1536]{1,0:T(4,128)(4,1)S(1)} %get-tuple-element.7, pred[4,1536]{1,0:T(4,128)(4,1)S(1)} %get-tuple-element.9), kind=kLoop, calls=%fused_computation.23 | loop fusion | flops 25165824 | bytes 50343936 | tf_op jit(solution)/shard_map/jit(_where)/select_n | solution.py:61
  347.7 0.1 reduce-scatter.4.cloned.1.call-update
  347.7 0.1 all-gather.3.cloned.1.call-start
  347.8 0.5 copy-done.12
  348.3 0.0 copy-done.13
  348.4 0.0 copy-done.14
  348.4 0.0 copy-done.15
  348.4 132.7 %reduce-scatter.4.cloned.1.call-done = bf16[4,192,2048]{2,1,0:T(8,128)(2,1)} async-done(((bf16[4,1536,2048]{2,1,0:T(8,128)(2,1)}), bf16[4,192,2048]{2,1,0:T(8,128)(2,1)}) %reduce-scatter.4.cloned.1.call-update) | async-done | bytes 3145744 | tf_op jit(solution)/shard_map/reduce_scatter | solution.py:62
  481.1 2.5 convert_reduce_fusion.2
  483.7 2.9 fusion.33
  486.6 0.0 copy-done.1
  486.6 0.0 copy-start.9
  486.6 1.4 convert_reduce_fusion.1
  488.0 0.0 copy-start.21
  488.0 0.0 copy-start.23
  488.0 0.0 copy-start.11
  488.0 2.0 fusion.29
  490.0 0.0 copy-done.3
  490.0 0.0 copy-done.5
  490.1 0.0 copy-done.7
  490.1 0.0 copy-done.9
  490.1 6.8 fusion.32
  496.9 0.1 all-gather.3.cloned.1.call-update
  497.0 0.1 reduce-scatter.6.cloned.1.call-start
  497.0 0.0 copy-done.21
  497.1 0.0 copy-done.23
  497.1 0.1 dynamic_slice.3
  497.2 0.0 copy-done.11
  497.2 1.3 subtract_convert_fusion
  498.5 1.3 iota_compare_fusion
  499.8 7.4 broadcast_multiply_fusion
  507.3 7.6 and_or_fusion
  514.8 100.5 %all-gather.3.cloned.1.call-done = bf16[4,1536,2048]{2,1,0:T(8,128)(2,1)} async-done(((bf16[4,192,2048]{2,1,0:T(8,128)(2,1)}), bf16[4,1536,2048]{2,1,0:T(8,128)(2,1)}) %all-gather.3.cloned.1.call-update) | async-done | bytes 25165840 | tf_op jit(solution)/shard_map/all_gather | solution.py:65
  615.3 26.5 %add_convert_fusion = bf16[4,1536,2,3,128]{4,1,3,2,0:T(8,128)(2,1)} fusion(f32[2,3,128]{2,1,0:T(4,128)S(1)} %copy.20, bf16[4,1536,2048]{2,1,0:T(8,128)(2,1)} %all-gather.3.cloned.1.call-done, bf16[2048,2,3,128]{3,1,2,0:T(2,128)(2,1)} %param.25), kind=kOutput, calls=%fused_computation.24 | convolution fusion | flops 19336790016 | bytes 37751808 | tf_op jit(solution)/shard_map/bsd,dhce->bshce/dot_general | solution.py:35
  641.8 54.2 %fusion.57 = (f32[4,2,1536]{2,1,0:T(2,128)S(1)}, f32[4,2,1536,1536]{2,3,1,0:T(8,128)}) fusion(f32[2,1536,1536]{1,2,0:T(8,128)} %broadcast_multiply_fusion, pred[4,1536,1536]{1,2,0:T(8,128)(4,1)} %and_or_fusion, bf16[4,1536,2,3,128]{4,1,3,2,0:T(8,128)(2,1)} %add_convert_fusion), kind=kOutput, calls=%fused_computation.87 | convolution fusion | flops 4926211584 | bytes 110149632 | tf_op jit(solution)/shard_map/sub | solution.py:46
  696.1 27.8 %fusion.45 = bf16[4,2,128,1536]{3,2,1,0:T(8,128)(2,1)} fusion(f32[4,2,1536,1536]{2,3,1,0:T(8,128)} %get-tuple-element.11, f32[4,2,1536]{2,1,0:T(2,128)S(1)} %get-tuple-element.10, bf16[4,1536,2,3,128]{4,1,3,2,0:T(8,128)(2,1)} %add_convert_fusion), kind=kOutput, calls=%fused_computation.62 | convolution fusion | flops 4871159808 | bytes 81838080 | tf_op jit(solution)/shard_map/bhqk,bkhd->bqhd/dot_general | solution.py:47
  723.8 0.0 copy-done
  723.8 13.6 %convolution_convert_fusion.1 = bf16[4,1536,2048]{2,1,0:T(8,128)(2,1)} fusion(bf16[4,1536,256]{1,2,0:T(8,128)(2,1)} %bitcast.55, bf16[256,2048]{1,0:T(8,128)(2,1)S(1)} %copy-done), kind=kOutput, calls=%fused_computation.14 | convolution fusion | flops 6455033856 | bytes 29360128 | tf_op jit(solution)/shard_map/bsf,fd->bsd/dot_general | solution.py:69
  737.5 0.1 reduce-scatter.6.cloned.1.call-update
  737.6 0.1 all-gather.5.cloned.1.call-start
  737.6 0.5 copy-done.16
  738.2 0.0 copy-done.17
  738.2 0.0 copy-done.18
  738.2 127.9 %reduce-scatter.6.cloned.1.call-done = bf16[4,192,2048]{2,1,0:T(8,128)(2,1)} async-done(((bf16[4,1536,2048]{2,1,0:T(8,128)(2,1)}), bf16[4,192,2048]{2,1,0:T(8,128)(2,1)}) %reduce-scatter.6.cloned.1.call-update) | async-done | bytes 3145744 | tf_op jit(solution)/shard_map/reduce_scatter | solution.py:70
  866.1 0.0 copy-done.6
  866.1 4.2 convert_reduce_fusion
  870.3 0.0 copy-start.2
  870.3 0.0 copy-start.20
  870.3 1.0 fusion.25
  871.3 0.6 copy-done.2
  872.0 2.9 fusion.28
  874.9 0.1 all-gather.5.cloned.1.call-update
  874.9 0.1 reduce-scatter.8.cloned.1.call-start
  875.0 118.3 %all-gather.5.cloned.1.call-done = bf16[4,1536,2048]{2,1,0:T(8,128)(2,1)} async-done(((bf16[4,192,2048]{2,1,0:T(8,128)(2,1)}), bf16[4,1536,2048]{2,1,0:T(8,128)(2,1)}) %all-gather.5.cloned.1.call-update) | async-done | bytes 25165840 | tf_op jit(solution)/shard_map/all_gather | solution.py:73
  993.3 39.1 %fusion.12.clone.4 = bf16[4,1536,1024]{2,1,0:T(8,128)(2,1)} fusion(bf16[4,1536,2048]{2,1,0:T(8,128)(2,1)} %all-gather.5.cloned.1.call-done, f32[1024]{0:T(1024)S(1)} %convert_element_type.112, bf16[2048,1024]{1,0:T(8,128)(2,1)} %param.31), kind=kOutput, calls=%fused_computation.20.clone.clone.clone.1 | convolution fusion | flops 25832718336 | bytes 41947136 | tf_op jit(solution)/shard_map/bsd,df->bsf/dot_general | solution.py:74
  1032.4 34.1 %convolution_convert_fusion = bf16[4,1536,2048]{2,1,0:T(8,128)(2,1)} fusion(bf16[1024,2048]{1,0:T(8,128)(2,1)S(1)} %copy-done.22, bf16[4,1536,1024]{2,1,0:T(8,128)(2,1)} %fusion.12.clone.4), kind=kOutput, calls=%fused_computation.13 | convolution fusion | flops 25782386688 | bytes 41943040 | tf_op jit(solution)/shard_map/bsf,fd->bsd/dot_general | solution.py:76
  1066.4 0.1 reduce-scatter.8.cloned.1.call-update
  1066.5 0.6 copy-done.19
  1067.1 127.9 %reduce-scatter.8.cloned.1.call-done = bf16[4,192,2048]{2,1,0:T(8,128)(2,1)} async-done(((bf16[4,1536,2048]{2,1,0:T(8,128)(2,1)}), bf16[4,192,2048]{2,1,0:T(8,128)(2,1)}) %reduce-scatter.8.cloned.1.call-update) | async-done | bytes 3145744 | tf_op jit(solution)/shard_map/reduce_scatter | solution.py:77
  1195.0 6.2 fusion.40
  (41 shorter events, 0.1 us)
Async XLA Ops:
  6.5 717.3 %copy-start = (bf16[256,2048]{1,0:T(8,128)(2,1)S(1)}, bf16[256,2048]{1,0:T(8,128)(2,1)}, u32[]{:S(2)}) copy-start(bf16[256,2048]{1,0:T(8,128)(2,1)} %param.27) | copy-start | bytes 3145732
  6.6 474.6 %reduce-scatter.4.cloned.1.call-start = ((), (), s32[]{:S(2)}) async-start(), calls=%async_computation.3 | async-start | bytes 28311552 | tf_op jit(solution)/shard_map/reduce_scatter | solution.py:62
  347.7 0.7 copy-start.12
  347.7 0.7 copy-start.13
  347.7 0.7 copy-start.14
  347.7 0.7 copy-start.15
  347.7 267.6 %all-gather.3.cloned.1.call-start = ((), (), s32[]{:S(2)}) async-start(), calls=%async_computation.4 | async-start | bytes 28311552 | tf_op jit(solution)/shard_map/all_gather | solution.py:65
  348.4 141.7 %copy-start.3 = (f32[2048]{0:T(1024)}, f32[2048]{0:T(1024)S(1)}, u32[]{:S(2)}) copy-start(f32[2048]{0:T(1024)S(1)} %convert_element_type.91) | copy-start | bytes 24580
  348.4 141.7 %copy-start.5 = (f32[2048]{0:T(1024)}, f32[2048]{0:T(1024)S(1)}, u32[]{:S(2)}) copy-start(f32[2048]{0:T(1024)S(1)} %convert_element_type.92) | copy-start | bytes 24580
  481.1 5.4 copy-start.1
  483.7 6.4 copy-start.7
  486.6 3.5 copy-start.9
  488.0 9.0 copy-start.21
  488.0 9.1 copy-start.23
  488.0 9.1 copy-start.11
  497.0 369.1 %reduce-scatter.6.cloned.1.call-start = ((), (), s32[]{:S(2)}) async-start(), calls=%async_computation.5 | async-start | bytes 28311552 | tf_op jit(solution)/shard_map/reduce_scatter | solution.py:70
  737.5 0.7 copy-start.16
  737.5 0.7 copy-start.17
  737.5 0.7 copy-start.18
  737.5 128.6 %copy-start.4 = (f32[2048]{0:T(1024)S(1)}, f32[2048]{0:T(1024)}, u32[]{:S(2)}) copy-start(f32[2048]{0:T(1024)} %copy-done.3) | copy-start | bytes 24580
  737.5 128.6 %copy-start.6 = (f32[2048]{0:T(1024)S(1)}, f32[2048]{0:T(1024)}, u32[]{:S(2)}) copy-start(f32[2048]{0:T(1024)} %copy-done.5) | copy-start | bytes 24580
  737.5 128.6 %copy-start.8 = (f32[4,192]{1,0:T(4,128)S(1)}, f32[4,192]{1,0:T(4,128)}, u32[]{:S(2)}) copy-start(f32[4,192]{1,0:T(4,128)} %copy-done.7) | copy-start | bytes 9220
  737.5 128.6 %copy-start.10 = (f32[4,192]{1,0:T(4,128)S(1)}, f32[4,192]{1,0:T(4,128)}, u32[]{:S(2)}) copy-start(f32[4,192]{1,0:T(4,128)} %copy-done.9) | copy-start | bytes 9220
  737.6 255.8 %all-gather.5.cloned.1.call-start = ((), (), s32[]{:S(2)}) async-start(), calls=%async_computation.6 | async-start | bytes 28311552 | tf_op jit(solution)/shard_map/all_gather | solution.py:73
  870.3 1.7 copy-start.2
  870.3 4.7 copy-start.20
  874.9 320.1 %reduce-scatter.8.cloned.1.call-start = ((), (), s32[]{:S(2)}) async-start(), calls=%async_computation.7 | async-start | bytes 28311552 | tf_op jit(solution)/shard_map/reduce_scatter | solution.py:77
  993.3 39.1 %copy-start.22 = (bf16[1024,2048]{1,0:T(8,128)(2,1)S(1)}, bf16[1024,2048]{1,0:T(8,128)(2,1)}, u32[]{:S(2)}) copy-start(bf16[1024,2048]{1,0:T(8,128)(2,1)} %param.33) | copy-start | bytes 12582916
  1066.4 0.7 copy-start.19
Sparse Core Ops, SparseCore 0:
  347.9 133.2 reduce-scatter.3
  497.1 118.2 all-gather.2
  737.7 128.3 reduce-scatter.5
  875.1 118.2 all-gather.4
  1066.6 128.3 reduce-scatter.7
where the time goes:
time: 1220 us; the launch traced here: 1210 us
  waiting for transfers between devices  608 us (50%)
  local copies, waits for them, and re-layouts  321 us (26%)
  matrix products  195 us (16%)
  other arithmetic  69.9 us (6%)
  between operations  13.9 us (1%)
    gather x1, local copies, waits for them, and re-layouts, local_step(): jnp.take(emb_shard, jnp.clip(local_ids, 0, vocab_loc - 1), axis=0)  319 us
    reduce_scatter x1, waiting for transfers between devices, local_step(): lax.psum_scatter(partial_emb, 'tp', scatter_dimension=1, tiled=True)  133 us
    reduce_scatter x1, waiting for transfers between devices, local_step(): lax.psum_scatter(attn_part, 'tp', scatter_dimension=1, tiled=True)  128 us
    reduce_scatter x1, waiting for transfers between devices, local_step(): lax.psum_scatter(down_part, 'tp', scatter_dimension=1, tiled=True)  128 us
    all_gather x1, waiting for transfers between devices, local_step(): normed2_all = lax.all_gather(normed2, 'tp', axis=1, tiled=True)  118 us
    all_gather x1, waiting for transfers between devices, local_step(): normed_all = lax.all_gather(normed, 'tp', axis=1, tiled=True)  100 us
    sub x1, matrix products, attention_block(): attn_probs = jax.nn.softmax(scores, axis=-1).astype(jnp.bfloat16)  54.2 us
    dot_general x1, matrix products, local_step(): jnp.einsum('bsd,df->bsf', normed2_all, w_up, preferred_element_type=jnp.f...  39.1 us
  transfers between devices with their start and end apart: 5, of which 5 were waited for; matrix products, arithmetic and copies ran while one was open for 1% of the time, Pallas kernels for 0%

commit v1 on v0

v1 whole, which is shorter than its diff:
```python
import functools
import math
import jax
import jax.numpy as jnp
from jax import lax
from jax.experimental import pallas as pl
from jax.experimental.pallas import tpu as pltpu
from jax.sharding import PartitionSpec as P

LN_EPS = 1e-5
BIAS_ROWS = 16


def alibi_slopes(n_heads):
    closest = 2 ** int(math.floor(math.log2(n_heads)))
    base_ratio = 2.0 ** (-(2.0 ** -(math.log2(closest) - 3)))
    extra_ratio = 2.0 ** (-(2.0 ** -(math.log2(2 * closest) - 3)))
    first_part = [base_ratio ** step_k for step_k in range(1, closest + 1)]
    second_part = [extra_ratio ** step_k for step_k in range(1, 2 * (n_heads - closest), 2)]
    return first_part + second_part


def layer_norm(values_in, ln_gain, ln_shift):
    values_in = values_in.astype(jnp.float32)
    mean_v = jnp.mean(values_in, axis=-1, keepdims=True)
    centered = values_in - mean_v
    var_v = jnp.mean(centered * centered, axis=-1, keepdims=True)
    scaled = centered * lax.rsqrt(var_v + LN_EPS)
    return (scaled * ln_gain.astype(jnp.float32) + ln_shift.astype(jnp.float32)).astype(jnp.bfloat16)


def bloom_gelu(values_in):
    return values_in * 0.5 * (1.0 + jnp.tanh(0.79788456 * values_in * (1.0 + 0.044715 * values_in * values_in)))


def attention_kernel(block, slope_ref, pad_ref, q_ref, k_ref, v_ref, out_ref):
    seq_len, head_dim = q_ref.shape
    slope = slope_ref[pl.program_id(0)]
    for first in range(0, seq_len, block):
        n_keys = first + block
        scores = lax.dot_general(q_ref[first:n_keys], k_ref[:n_keys], (((1,), (1,)), ((), ())), preferred_element_type=jnp.float32)
        key_pos = lax.broadcasted_iota(jnp.int32, (block, n_keys), 1)
        query_pos = lax.broadcasted_iota(jnp.int32, (block, n_keys), 0) + first
        distance = key_pos - query_pos
        scores = scores * (head_dim ** -0.5) + slope * distance.astype(jnp.float32)
        allowed = ((distance <= 0) & (pad_ref[:, :n_keys] == 1)) | (distance == 0)
        scores = jnp.where(allowed, scores, -1e30)
        weights = jnp.exp(scores - jnp.max(scores, axis=-1, keepdims=True))
        probs = (weights / jnp.sum(weights, axis=-1, keepdims=True)).astype(jnp.bfloat16)
        out_ref[first:n_keys] = jnp.dot(probs, v_ref[:n_keys], preferred_element_type=jnp.float32).astype(jnp.bfloat16)


def attention(qkv, pad_mask, slopes, heads, head_dim):
    n_seq, seq_len, _ = qkv.shape
    block = math.gcd(seq_len, 256)
    column = lambda part: pl.BlockSpec((None, seq_len, head_dim), lambda h, b: (b, 0, 3 * h + part))
    return pl.pallas_call(
        functools.partial(attention_kernel, block),
        grid=(heads, n_seq),
        in_specs=[pl.BlockSpec(memory_space=pltpu.SMEM), pl.BlockSpec((None, 1, seq_len), lambda h, b: (b, 0, 0)), column(0), column(1), column(2)],
        out_specs=pl.BlockSpec((None, seq_len, head_dim), lambda h, b: (b, 0, h)),
        out_shape=jax.ShapeDtypeStruct((n_seq, seq_len, heads * head_dim), jnp.bfloat16),
        cost_estimate=pl.CostEstimate(flops=4 * n_seq * heads * seq_len * seq_len * head_dim, bytes_accessed=qkv.size * 3, transcendentals=n_seq * heads * seq_len * seq_len // 2),
        name='attention',
    )(slopes, pad_mask[:, None], qkv, qkv, qkv)


def mlp_kernel(row_block, normed_ref, up_ref, down_ref, resid_ref, shift_ref, out_ref, total):
    step = pl.program_id(0)
    rows, width = normed_ref.shape
    up = up_ref[...].reshape(width, up_ref.shape[-1])
    down_rows = down_ref.shape[1] - BIAS_ROWS
    down = down_ref[:, :down_rows].reshape(-1, down_ref.shape[-1])
    bias = down_ref[0, down_rows:, :up.shape[1]][:1].astype(jnp.float32)
    for first in range(0, rows, row_block):
        part = slice(first, first + row_block)
        hidden = jnp.dot(normed_ref[part], up, preferred_element_type=jnp.float32) + bias
        activated = bloom_gelu(hidden).astype(jnp.bfloat16)
        product = jnp.dot(activated, down, preferred_element_type=jnp.float32)

        @pl.when(step == 0)
        def _():
            total[part] = product

        @pl.when(step > 0)
        def _():
            total[part] += product

    @pl.when(step == pl.num_programs(0) - 1)
    def _():
        out_ref[...] = (resid_ref[...].astype(jnp.float32) + total[...] + shift_ref[...].astype(jnp.float32)).astype(jnp.bfloat16)


def mlp(normed, up_all, down_all, resid, shift):
    rows, width = normed.shape
    n_dp, n_tp, up_rows, hidden = up_all.shape
    whole = lambda t: (0, 0)
    return pl.pallas_call(
        functools.partial(mlp_kernel, math.gcd(rows, 256)),
        grid=(n_tp,),
        in_specs=[
            pl.BlockSpec((rows, width), whole),
            pl.BlockSpec((n_dp, None, up_rows, hidden), lambda t: (0, t, 0, 0)),
            pl.BlockSpec((n_dp, None, down_all.shape[2], width), lambda t: (0, t, 0, 0)),
            pl.BlockSpec((rows, width), whole),
            pl.BlockSpec((1, width), whole),
        ],
        out_specs=pl.BlockSpec((rows, width), whole),
        out_shape=jax.ShapeDtypeStruct((rows, width), jnp.bfloat16),
        scratch_shapes=[pltpu.VMEM((rows, width), jnp.float32)],
        compiler_params=pltpu.CompilerParams(vmem_limit_bytes=60 * 1024 * 1024),
        cost_estimate=pl.CostEstimate(flops=4 * rows * width * hidden * n_tp, bytes_accessed=2 * (up_all.size + down_all.size), transcendentals=rows * hidden * n_tp),
        name='mlp',
    )(normed, up_all, down_all, resid, shift)


def solution(mesh):
    n_tp, n_dp = mesh.shape['tp'], mesh.shape['dp']

    def gather_weight(shard, extra=None):
        rows = shard.shape[0] // n_dp
        part = lax.dynamic_slice_in_dim(shard, lax.axis_index('dp') * rows, rows)
        if extra is not None:
            part = jnp.concatenate([part, jnp.pad(extra[None], ((0, BIAS_ROWS - 1), (0, shard.shape[1] - extra.shape[0])))])
        return lax.all_gather(part, ('dp', 'tp'), axis=0, tiled=True).reshape(n_dp, n_tp, part.shape[0], shard.shape[1])

    def local_step(tok_ids, pad_mask, emb_shard, ln_emb_w, ln_emb_b, ln1_w, ln1_b, w_qkv, b_qkv, w_out, b_out, ln2_w, ln2_b, w_up, b_up, w_down, b_down):
        tp_rank = lax.axis_index('tp')
        vocab_loc, width = emb_shard.shape
        heads_loc, head_dim = w_qkv.shape[1], w_qkv.shape[3]
        n_seq, seq_len = tok_ids.shape
        seq_loc = seq_len // n_tp
        up_all, down_all, out_all = gather_weight(w_up), gather_weight(w_down, b_up), gather_weight(w_out)
        all_slopes = jnp.array(alibi_slopes(heads_loc * n_tp), jnp.float32)
        head_slopes = lax.dynamic_slice_in_dim(all_slopes, tp_rank * heads_loc, heads_loc)
        local_ids = tok_ids - tp_rank * vocab_loc
        in_range = (local_ids >= 0) & (local_ids < vocab_loc)
        looked_up = jnp.take(emb_shard, jnp.clip(local_ids, 0, vocab_loc - 1), axis=0)
        partial_emb = jnp.where(in_range[:, :, None], looked_up, jnp.zeros((), jnp.bfloat16))
        partial_emb, up_all, down_all, out_all = lax.optimization_barrier((partial_emb, up_all, down_all, out_all))
        out_all = out_all.transpose(1, 0, 2, 3).reshape(-1, width)
        embedded = lax.psum_scatter(partial_emb, 'tp', scatter_dimension=1, tiled=True)
        resid_in = layer_norm(embedded, ln_emb_w, ln_emb_b)
        normed = layer_norm(resid_in, ln1_w, ln1_b)
        normed_all = lax.all_gather(normed, 'tp', axis=1, tiled=True)
        qkv = (jnp.einsum('bsd,de->bse', normed_all, w_qkv.reshape(width, -1), preferred_element_type=jnp.float32) + b_qkv.reshape(-1).astype(jnp.float32)).astype(jnp.bfloat16)
        context = attention(qkv, pad_mask, head_slopes, heads_loc, head_dim)
        context = lax.all_to_all(context.reshape(n_seq, n_tp, seq_loc, heads_loc * head_dim), 'tp', 1, 3, tiled=True).reshape(n_seq * seq_loc, width)
        attn_proj = jnp.dot(context, out_all, preferred_element_type=jnp.float32)
        resid_mid = (resid_in.reshape(-1, width).astype(jnp.float32) + attn_proj + b_out.astype(jnp.float32)).astype(jnp.bfloat16)
        normed2 = layer_norm(resid_mid, ln2_w, ln2_b)
        out = mlp(normed2, up_all, down_all, resid_mid, b_down[None])
        return out.reshape(n_seq, seq_loc, width)

    replicated = P(None)
    in_specs = (P('dp', None), P('dp', None), P('tp', None), replicated, replicated, replicated, replicated, P(None, 'tp', None, None), P('tp', None, None), P('tp', None), replicated, replicated, replicated, P(None, 'tp'), P('tp'), P('tp', None), replicated)
    return jax.shard_map(local_step, mesh=mesh, in_specs=in_specs, out_specs=P('dp', 'tp', None), check_vma=False)
```

time: 1220 us -> 902 us (0.74)
  waiting for transfers between devices: 608 us -> 345 us
  matrix products: 195 us -> 33.7 us
  Pallas kernels: 0 us -> 107 us
  local copies, waits for them, and re-layouts: 321 us -> 355 us
  other arithmetic: 69.9 us -> 37.4 us
    reduce_scatter x2 -> x0, waiting for transfers between devices: 256 us -> none  [the longest x1 128 us: local_step(): lax.psum_scatter(attn_part, 'tp', scatter_dimension=1, tiled=True)]
    dot_general x5 -> x2, matrix products: 141 us -> 33.7 us  [the longest x1 26.4 us: local_step(): jnp.einsum('bsd,de->bse', normed_all, w_qkv.reshape(width, -1), preferred...]
    pallas_call x0 -> x2, Pallas kernels: none -> 107 us  [the longest x1 71.3 us: mlp(): pl.pallas_call(functools.partial(mlp_kernel, math.gcd(rows, 256)), grid=(...]
    sub x1 -> x0, matrix products: 54.2 us -> none  [attention_block(): attn_probs = jax.nn.softmax(scores, axis=-1).astype(jnp.bfloat16)]
    all_gather x1 -> x3, waiting for transfers between devices: 118 us -> 80.2 us  [gather_weight(): lax.all_gather(part, ('dp', 'tp'), axis=0, tiled=True)]
    all_to_all x0 -> x1, waiting for transfers between devices: none -> 28.3 us  [local_step(): lax.all_to_all(context.reshape(n_seq, n_tp, seq_loc, heads_loc * head_dim...]
  transfers between devices with their start and end apart: 5 -> 6, of which waited for: 5 -> 4; matrix products, arithmetic and copies ran while one was open for 1% -> 41% of each run, Pallas kernels for 0% -> 0%
where the time goes in v1:
time: 902 us; the launch traced here: 895 us
  local copies, waits for them, and re-layouts  355 us (39%)
  waiting for transfers between devices  345 us (38%)
  Pallas kernels  107 us (12%)
  other arithmetic  37.4 us (4%)
  matrix products  33.7 us (4%)
  between operations  13.4 us (1%)
    gather x1, local copies, waits for them, and re-layouts, local_step(): jnp.take(emb_shard, jnp.clip(local_ids, 0, vocab_loc - 1), axis=0)  319 us
    reduce_scatter x1, waiting for transfers between devices, local_step(): lax.psum_scatter(partial_emb, 'tp', scatter_dimension=1, tiled=True)  127 us
    all_gather x1, waiting for transfers between devices, local_step(): normed_all = lax.all_gather(normed, 'tp', axis=1, tiled=True)  108 us
    all_gather x3, waiting for transfers between devices, gather_weight(): lax.all_gather(part, ('dp', 'tp'), axis=0, tiled=True)  80.2 us
    pallas_call x1, Pallas kernels, mlp(): pl.pallas_call(functools.partial(mlp_kernel, math.gcd(rows, 256)), grid=(...  71.3 us
    pallas_call x1, Pallas kernels, attention(): pl.pallas_call(functools.partial(attention_kernel, block), grid=(heads, n...  35.4 us
    all_to_all x1, waiting for transfers between devices, local_step(): lax.all_to_all(context.reshape(n_seq, n_tp, seq_loc, heads_loc * head_dim...  28.3 us
    dot_general x1, matrix products, local_step(): jnp.einsum('bsd,de->bse', normed_all, w_qkv.reshape(width, -1), preferred...  26.4 us
  transfers between devices with their start and end apart: 6, of which 4 were waited for; matrix products, arithmetic and copies ran while one was open for 41% of the time, Pallas kernels for 0%

profile of v1, /device:TPU:81, one launch (start us, length us, event | category | flops | bytes accessed | tf_op | source)
XLA Modules:
  0.0 895.4 jit_solution(7932883616441607453)
XLA Ops:
  6.5 0.0 copy-start
  6.6 0.0 all-gather.9.cloned.1.call-start
  6.6 1.2 copy-done
  7.8 0.7 constant_dynamic-slice_fusion
  8.5 0.1 all-gather.9.cloned.1.call-update
  8.6 0.1 all-gather.5.cloned.1.call-start
  8.6 2.3 constant_dynamic-slice_fusion.2
  10.9 0.1 all-gather.5.cloned.1.call-update
  11.0 0.1 all-gather.7.cloned.1.call-start
  11.0 0.7 broadcast_in_dim.53
  11.7 1.3 constant_dynamic-slice_fusion.1
  13.1 1.1 fusion.15
  14.2 0.1 all-gather.7.cloned.1.call-update
  14.2 0.1 reduce-scatter.2.cloned.1.call-start
  14.3 0.0 copy-done.8
  14.4 318.6 %gather_fusion = bf16[6144,2048]{1,0:T(8,128)(2,1)} fusion(bf16[31360,2048]{1,0:T(8,128)(2,1)} %param.20, s32[6144]{0:T(1024)S(1)} %broadcast_clamp_fusion), kind=kCustom, calls=%fused_computation | custom fusion | bytes 50356224 | tf_op jit(solution)/shard_map/jit(_take)/gather | solution.py:138
  333.0 21.4 %select_select_fusion = bf16[4,1536,2048]{2,1,0:T(8,128)(2,1)} fusion(bf16[4,1536,2048]{2,1,0:T(8,128)(2,1)} %bitcast.28, pred[4,1536]{1,0:T(4,128)(4,1)S(1)} %get-tuple-element.15, pred[4,1536]{1,0:T(4,128)(4,1)S(1)} %get-tuple-element.17), kind=kLoop, calls=%fused_computation.1 | loop fusion | flops 25165824 | bytes 50343936 | tf_op jit(solution)/shard_map/jit(_where)/select_n | solution.py:139
  354.4 80.2 %all-gather.7.cloned.1.call-done = bf16[8704,2048]{1,0:T(8,128)(2,1)} async-done(((bf16[272,2048]{1,0:T(8,128)(2,1)}), bf16[8704,2048]{1,0:T(8,128)(2,1)}) %all-gather.7.cloned.1.call-update) | async-done | bytes 35651600 | tf_op jit(solution)/shard_map/all_gather | solution.py:125
  434.6 0.1 reduce-scatter.2.cloned.1.call-update
  434.7 0.2 all-gather.11.cloned.1.call-start
  434.9 0.4 copy-done.9
  435.3 0.0 copy-done.10
  435.3 0.0 copy-done.11
  435.3 0.0 copy-done.12
  435.3 127.5 %reduce-scatter.2.cloned.1.call-done = bf16[4,192,2048]{2,1,0:T(8,128)(2,1)} async-done(((bf16[4,1536,2048]{2,1,0:T(8,128)(2,1)}), bf16[4,192,2048]{2,1,0:T(8,128)(2,1)}) %reduce-scatter.2.cloned.1.call-update) | async-done | bytes 3145744 | tf_op jit(solution)/shard_map/reduce_scatter | solution.py:142
  562.8 2.5 convert_reduce_fusion.1
  565.4 2.9 fusion.8
  568.2 0.0 copy-done.4
  568.3 1.7 convert_reduce_fusion.2
  570.0 0.0 copy-start.2
  570.0 0.0 copy-start.7
  570.0 1.0 multiply_reduce_fusion
  571.0 0.6 copy-done.2
  571.6 2.9 add_convert_fusion.1
  574.5 0.1 all-gather.11.cloned.1.call-update
  574.6 0.0 copy-done.7
  574.6 0.6 broadcast_in_dim.54.pad_ref
  575.2 8.7 copy.28
  583.9 0.0 copy-done.17
  584.0 0.0 copy-done.18
  584.0 0.6 dynamic_slice.15.slope_ref
  584.6 108.4 %all-gather.11.cloned.1.call-done = bf16[4,1536,2048]{2,1,0:T(8,128)(2,1)} async-done(((bf16[4,192,2048]{2,1,0:T(8,128)(2,1)}), bf16[4,1536,2048]{2,1,0:T(8,128)(2,1)}) %all-gather.11.cloned.1.call-update) | async-done | bytes 25165840 | tf_op jit(solution)/shard_map/all_gather | solution.py:145
  692.9 26.4 %add_convert_fusion.q_ref.k_ref.v_ref = bf16[4,1536,768]{2,1,0:T(8,128)(2,1)} fusion(bf16[4,1536,2048]{2,1,0:T(8,128)(2,1)} %all-gather.11.cloned.1.call-done, bf16[2048,768,1]{0,1,2:T(8,128)(2,1)} %bitcast.32, f32[768]{0:T(1024)S(1)} %reshape.94), kind=kOutput, calls=%fused_computation.2 | convolution fusion | flops 19336790016 | bytes 37751808 | tf_op jit(solution)/shard_map/bsd,de->bse/dot_general | solution.py:146
  719.4 35.4 %attention.1 = bf16[4,1536,256]{2,1,0:T(8,128)(2,1)} custom-call(f32[2]{0:T(128)} %dynamic_slice.15.slope_ref, s32[4,1,1536]{2,1,0:T(1,128)} %broadcast_in_dim.54.pad_ref, bf16[4,1536,768]{2,1,0:T(8,128)(2,1)} %add_convert_fusion.q_ref.k_ref.v_ref, bf16[4,1536,768]{2,1,0:T(8,128)(2,1)} %add_convert_fusion.q_ref.k_ref.v_ref, ...), custom_call_target="tpu_custom_call" | custom-call | flops 9663676416 | bytes 14155776 | tf_op jit(solution)/shard_map/attention/pallas_call | solution.py:57
  754.7 0.0 copy-start.15
  754.8 0.0 copy-start.16
  754.8 3.9 copy.31
  758.7 4.5 all-to-all-start
  763.2 0.0 copy-done.13
  763.2 0.0 copy-done.14
  763.2 0.0 copy-done.15
  763.2 0.0 copy-done.16
  763.2 0.6 broadcast_in_dim.55.shift_ref
  763.8 8.4 copy.33
  772.2 28.3 %all-to-all-done = bf16[4,8,192,256]{3,2,0,1:T(8,128)(2,1)} async-done(((bf16[4,8,192,256]{3,2,0,1:T(8,128)(2,1)}), bf16[4,8,192,256]{3,2,0,1:T(8,128)(2,1)}, u32[]{:S(2)}, u32[]{:S(2)}) %all-to-all-start) | async-done | bytes 3145760 | tf_op jit(solution)/shard_map/all_to_all | solution.py:148
  800.5 3.8 copy.32
  804.3 1.1 copy.36
  805.5 0.0 copy-done.3
  805.5 0.3 copy-done.6
  805.8 7.2 convert_reduce_fusion
  813.0 1.0 fusion.4
  814.0 0.7 copy-done.5
  814.7 2.9 fusion.7.normed_ref
  817.6 71.3 %mlp.1 = bf16[768,2048]{1,0:T(8,128)(2,1)} custom-call(bf16[768,2048]{1,0:T(8,128)(2,1)} %fusion.7.normed_ref, bf16[4,8,512,1024]{3,2,1,0:T(8,128)(2,1)} %bitcast.36, bf16[4,8,272,2048]{3,2,1,0:T(8,128)(2,1)} %bitcast.35, bf16[768,2048]{1,0:T(8,128)(2,1)} %copy-done.5, bf16[1,2048]{1,0:T(2,128)(2,1)} %broadcast_in_dim.55.shift_ref), custom_call_target="tpu_custom_call" | custom-call | flops 51539607552 | bytes 69206016 | tf_op jit(solution)/shard_map/mlp/pallas_call | solution.py:98
  (35 shorter events, 0.2 us)
Async XLA Ops:
  6.5 1.2 copy-start
  6.6 7.8 copy-start.8
  6.6 347.8 %all-gather.9.cloned.1.call-start = ((), (), s32[]{:S(2)}) async-start(), calls=%async_computation.4 | async-start | bytes 8650752 | tf_op jit(solution)/shard_map/all_gather | solution.py:125
  8.6 345.8 %all-gather.5.cloned.1.call-start = ((), (), s32[]{:S(2)}) async-start(), calls=%async_computation.2 | async-start | bytes 34603008 | tf_op jit(solution)/shard_map/all_gather | solution.py:125
  11.0 423.6 %all-gather.7.cloned.1.call-start = ((), (), s32[]{:S(2)}) async-start(), calls=%async_computation.3 | async-start | bytes 36765696 | tf_op jit(solution)/shard_map/all_gather | solution.py:125
  14.2 548.6 %reduce-scatter.2.cloned.1.call-start = ((), (), s32[]{:S(2)}) async-start(), calls=%async_computation.5 | async-start | bytes 28311552 | tf_op jit(solution)/shard_map/reduce_scatter | solution.py:142
  434.6 0.7 copy-start.9
  434.6 0.7 copy-start.10
  434.6 0.7 copy-start.11
  434.6 0.7 copy-start.12
  434.7 258.3 %all-gather.11.cloned.1.call-start = ((), (), s32[]{:S(2)}) async-start(), calls=%async_computation.6 | async-start | bytes 28311552 | tf_op jit(solution)/shard_map/all_gather | solution.py:145
  562.8 5.4 copy-start.4
  570.0 1.6 copy-start.2
  570.0 4.6 copy-start.7
  574.5 9.5 %copy-start.17 = (bf16[2,3,128]{2,0,1:T(2,128)(2,1)S(1)}, bf16[2,3,128]{2,0,1:T(2,128)(2,1)}, u32[]{:S(2)}) copy-start(bf16[2,3,128]{2,0,1:T(2,128)(2,1)} %param.26) | copy-start | bytes 4612
  574.5 9.5 %copy-start.18 = (f32[16]{0:T(128)S(1)}, f32[16]{0:T(128)}, u32[]{:S(2)}) copy-start(f32[16]{0:T(128)} %constant.62.clone) | copy-start | bytes 196
  754.7 8.4 copy-start.13
  754.7 8.5 copy-start.14
  754.7 8.5 copy-start.15
  754.8 8.5 copy-start.16
  758.7 41.8 %all-to-all-start = ((bf16[4,8,192,256]{3,2,0,1:T(8,128)(2,1)}), bf16[4,8,192,256]{3,2,0,1:T(8,128)(2,1)}, u32[]{:S(2)}, u32[]{:S(2)}) async-start(bf16[4,8,192,256]{3,2,0,1:T(8,128)(2,1)} %copy.31), calls=%async_computation.1 | async-start | bytes 6291456 | tf_op jit(solution)/shard_map/all_to_all | solution.py:148
  800.5 5.0 copy-start.3
  800.5 5.3 copy-start.6
  813.0 1.7 copy-start.5
  817.6 71.3 %copy-start.1 = (bf16[256,2048]{1,0:T(8,128)(2,1)S(1)}, bf16[256,2048]{1,0:T(8,128)(2,1)}, u32[]{:S(2)}) copy-start(bf16[256,2048]{1,0:T(8,128)(2,1)} %param.27) | copy-start | bytes 3145732
Sparse Core Ops, SparseCore 0:
  10.4 78.9 all-gather.8
  92.4 166.2 all-gather.4
  261.7 172.8 all-gather.6
  436.8 125.9 reduce-scatter.1
  574.7 118.2 all-gather.10

commit v2 on v1

--- a/solution.py
+++ b/solution.py
@@ -65,18 +65,38 @@
     )(slopes, pad_mask[:, None], qkv, qkv, qkv)
 
 
-def mlp_kernel(row_block, normed_ref, up_ref, down_ref, resid_ref, shift_ref, out_ref, total):
-    step = pl.program_id(0)
+def up_kernel(row_block, normed_ref, up_ref, out_ref):
     rows, width = normed_ref.shape
-    up = up_ref[...].reshape(width, up_ref.shape[-1])
-    down_rows = down_ref.shape[1] - BIAS_ROWS
-    down = down_ref[:, :down_rows].reshape(-1, down_ref.shape[-1])
-    bias = down_ref[0, down_rows:, :up.shape[1]][:1].astype(jnp.float32)
+    up_rows = up_ref.shape[1] - BIAS_ROWS
+    up = up_ref[:, :up_rows].reshape(width, up_ref.shape[-1])
+    bias = up_ref[0, up_rows:][:1].astype(jnp.float32)
     for first in range(0, rows, row_block):
         part = slice(first, first + row_block)
         hidden = jnp.dot(normed_ref[part], up, preferred_element_type=jnp.float32) + bias
-        activated = bloom_gelu(hidden).astype(jnp.bfloat16)
-        product = jnp.dot(activated, down, preferred_element_type=jnp.float32)
+        out_ref[part] = bloom_gelu(hidden).astype(jnp.bfloat16)
+
+
+def mlp_up(normed, up_all):
+    rows, width = normed.shape
+    n_dp, n_tp, up_rows, hidden = up_all.shape
+    return pl.pallas_call(
+        functools.partial(up_kernel, math.gcd(rows, 256)),
+        grid=(n_tp,),
+        in_specs=[pl.BlockSpec((rows, width), lambda t: (0, 0)), pl.BlockSpec((n_dp, None, up_rows, hidden), lambda t: (0, t, 0, 0))],
+        out_specs=pl.BlockSpec((rows, hidden), lambda t: (0, t)),
+        out_shape=jax.ShapeDtypeStruct((rows, hidden * n_tp), jnp.bfloat16),
+        compiler_params=pltpu.CompilerParams(vmem_limit_bytes=56 * 1024 * 1024),
+        cost_estimate=pl.CostEstimate(flops=2 * rows * width * hidden * n_tp, bytes_accessed=2 * up_all.size, transcendentals=rows * hidden * n_tp),
+        name='mlp_up',
+    )(normed, up_all)
+
+
+def down_kernel(row_block, act_ref, down_ref, resid_ref, shift_ref, out_ref, total):
+    step = pl.program_id(0)
+    down = down_ref[...].reshape(-1, down_ref.shape[-1])
+    for first in range(0, act_ref.shape[0], row_block):
+        part = slice(first, first + row_block)
+        product = jnp.dot(act_ref[part], down, preferred_element_type=jnp.float32)
 
         @pl.when(step == 0)
         def _():
@@ -91,27 +111,26 @@
         out_ref[...] = (resid_ref[...].astype(jnp.float32) + total[...] + shift_ref[...].astype(jnp.float32)).astype(jnp.bfloat16)
 
 
-def mlp(normed, up_all, down_all, resid, shift):
-    rows, width = normed.shape
-    n_dp, n_tp, up_rows, hidden = up_all.shape
+def mlp_down(activated, down_all, resid, shift):
+    rows, width = resid.shape
+    n_dp, n_tp, down_rows, _ = down_all.shape
     whole = lambda t: (0, 0)
     return pl.pallas_call(
-        functools.partial(mlp_kernel, math.gcd(rows, 256)),
+        functools.partial(down_kernel, math.gcd(rows, 256)),
         grid=(n_tp,),
         in_specs=[
-            pl.BlockSpec((rows, width), whole),
-            pl.BlockSpec((n_dp, None, up_rows, hidden), lambda t: (0, t, 0, 0)),
-            pl.BlockSpec((n_dp, None, down_all.shape[2], width), lambda t: (0, t, 0, 0)),
+            pl.BlockSpec((rows, n_dp * down_rows), lambda t: (0, t)),
+            pl.BlockSpec((n_dp, None, down_rows, width), lambda t: (0, t, 0, 0)),
             pl.BlockSpec((rows, width), whole),
             pl.BlockSpec((1, width), whole),
         ],
         out_specs=pl.BlockSpec((rows, width), whole),
         out_shape=jax.ShapeDtypeStruct((rows, width), jnp.bfloat16),
         scratch_shapes=[pltpu.VMEM((rows, width), jnp.float32)],
-        compiler_params=pltpu.CompilerParams(vmem_limit_bytes=60 * 1024 * 1024),
-        cost_estimate=pl.CostEstimate(flops=4 * rows * width * hidden * n_tp, bytes_accessed=2 * (up_all.size + down_all.size), transcendentals=rows * hidden * n_tp),
-        name='mlp',
-    )(normed, up_all, down_all, resid, shift)
+        compiler_params=pltpu.CompilerParams(vmem_limit_bytes=56 * 1024 * 1024),
+        cost_estimate=pl.CostEstimate(flops=2 * rows * width * n_dp * down_rows * n_tp, bytes_accessed=2 * down_all.size, transcendentals=0),
+        name='mlp_down',
+    )(activated, down_all, resid, shift)
 
 
 def solution(mesh):
@@ -130,26 +149,27 @@
         heads_loc, head_dim = w_qkv.shape[1], w_qkv.shape[3]
         n_seq, seq_len = tok_ids.shape
         seq_loc = seq_len // n_tp
-        up_all, down_all, out_all = gather_weight(w_up), gather_weight(w_down, b_up), gather_weight(w_out)
+        up_all, out_all = gather_weight(w_up, b_up), gather_weight(w_out)
         all_slopes = jnp.array(alibi_slopes(heads_loc * n_tp), jnp.float32)
         head_slopes = lax.dynamic_slice_in_dim(all_slopes, tp_rank * heads_loc, heads_loc)
         local_ids = tok_ids - tp_rank * vocab_loc
         in_range = (local_ids >= 0) & (local_ids < vocab_loc)
         looked_up = jnp.take(emb_shard, jnp.clip(local_ids, 0, vocab_loc - 1), axis=0)
         partial_emb = jnp.where(in_range[:, :, None], looked_up, jnp.zeros((), jnp.bfloat16))
-        partial_emb, up_all, down_all, out_all = lax.optimization_barrier((partial_emb, up_all, down_all, out_all))
+        partial_emb, up_all, out_all = lax.optimization_barrier((partial_emb, up_all, out_all))
         out_all = out_all.transpose(1, 0, 2, 3).reshape(-1, width)
         embedded = lax.psum_scatter(partial_emb, 'tp', scatter_dimension=1, tiled=True)
         resid_in = layer_norm(embedded, ln_emb_w, ln_emb_b)
         normed = layer_norm(resid_in, ln1_w, ln1_b)
-        normed_all = lax.all_gather(normed, 'tp', axis=1, tiled=True)
+        normed_all, down_shard = lax.optimization_barrier((lax.all_gather(normed, 'tp', axis=1, tiled=True), w_down))
+        down_all = gather_weight(down_shard)
         qkv = (jnp.einsum('bsd,de->bse', normed_all, w_qkv.reshape(width, -1), preferred_element_type=jnp.float32) + b_qkv.reshape(-1).astype(jnp.float32)).astype(jnp.bfloat16)
         context = attention(qkv, pad_mask, head_slopes, heads_loc, head_dim)
         context = lax.all_to_all(context.reshape(n_seq, n_tp, seq_loc, heads_loc * head_dim), 'tp', 1, 3, tiled=True).reshape(n_seq * seq_loc, width)
         attn_proj = jnp.dot(context, out_all, preferred_element_type=jnp.float32)
         resid_mid = (resid_in.reshape(-1, width).astype(jnp.float32) + attn_proj + b_out.astype(jnp.float32)).astype(jnp.bfloat16)
         normed2 = layer_norm(resid_mid, ln2_w, ln2_b)
-        out = mlp(normed2, up_all, down_all, resid_mid, b_down[None])
+        out = mlp_down(mlp_up(normed2, up_all), down_all, resid_mid, b_down[None])
         return out.reshape(n_seq, seq_loc, width)
 
     replicated = P(None)

time: 902 us -> 870 us (0.965)
  waiting for transfers between devices: 345 us -> 306 us
    all_gather x3, waiting for transfers between devices: 80.2 us -> 0.01 us  [gather_weight(): lax.all_gather(part, ('dp', 'tp'), axis=0, tiled=True)]
    all_to_all x1, waiting for transfers between devices: 28.3 us -> 54.4 us  [local_step(): lax.all_to_all(context.reshape(n_seq, n_tp, seq_loc, heads_loc * head_dim...]
    all_gather x1, waiting for transfers between devices: 108 us -> 118 us  [local_step(): lax.all_gather(normed, 'tp', axis=1, tiled=True)]
    pallas_call x1 -> x2, Pallas kernels: 71.3 us -> 77 us  [the longest x1 41.1 us: mlp_down(): pl.pallas_call(functools.partial(down_kernel, math.gcd(rows, 256)), grid=...]
  transfers between devices with their start and end apart: 6 -> 6, of which waited for: 4 -> 3; matrix products, arithmetic and copies ran while one was open for 41% -> 47% of each run, Pallas kernels for 0% -> 8%
where the time goes in v2:
time: 870 us; the launch traced here: 864 us
  local copies, waits for them, and re-layouts  355 us (41%)
  waiting for transfers between devices  306 us (35%)
  Pallas kernels  112 us (13%)
  other arithmetic  38.1 us (4%)
  matrix products  33.8 us (4%)
  between operations  13.4 us (2%)
    gather x1, local copies, waits for them, and re-layouts, local_step(): jnp.take(emb_shard, jnp.clip(local_ids, 0, vocab_loc - 1), axis=0)  319 us
    reduce_scatter x1, waiting for transfers between devices, local_step(): lax.psum_scatter(partial_emb, 'tp', scatter_dimension=1, tiled=True)  133 us
    all_gather x1, waiting for transfers between devices, local_step(): lax.all_gather(normed, 'tp', axis=1, tiled=True)  118 us
    all_to_all x1, waiting for transfers between devices, local_step(): lax.all_to_all(context.reshape(n_seq, n_tp, seq_loc, heads_loc * head_dim...  54.4 us
    pallas_call x1, Pallas kernels, mlp_down(): pl.pallas_call(functools.partial(down_kernel, math.gcd(rows, 256)), grid=...  41.1 us
    pallas_call x1, Pallas kernels, mlp_up(): pl.pallas_call(functools.partial(up_kernel, math.gcd(rows, 256)), grid=(n...  35.9 us
    pallas_call x1, Pallas kernels, attention(): pl.pallas_call(functools.partial(attention_kernel, block), grid=(heads, n...  35.4 us
    dot_general x1, matrix products, local_step(): jnp.einsum('bsd,de->bse', normed_all, w_qkv.reshape(width, -1), preferred...  26.6 us
  transfers between devices with their start and end apart: 6, of which 3 were waited for; matrix products, arithmetic and copies ran while one was open for 47% of the time, Pallas kernels for 8%

profile of v2, /device:TPU:81, one launch (start us, length us, event | category | flops | bytes accessed | tf_op | source)
XLA Modules:
  0.0 863.9 jit_solution(10916213325822755138)
XLA Ops:
  6.5 0.0 copy-start
  6.6 0.0 all-gather.7.cloned.1.call-start
  6.6 1.2 copy-done
  7.8 0.7 constant_dynamic-slice_fusion.1
  8.5 0.1 all-gather.7.cloned.1.call-update
  8.6 0.1 all-gather.5.cloned.1.call-start
  8.7 0.7 broadcast_in_dim.53
  9.3 1.3 constant_dynamic-slice_fusion.2
  10.6 1.1 fusion.15
  11.7 0.1 all-gather.5.cloned.1.call-update
  11.8 0.1 reduce-scatter.2.cloned.1.call-start
  11.8 0.8 compare_and_fusion
  12.7 318.8 %gather_fusion = bf16[6144,2048]{1,0:T(8,128)(2,1)} fusion(bf16[31360,2048]{1,0:T(8,128)(2,1)} %param.20, s32[6144]{0:T(1024)S(1)} %broadcast_clamp_fusion), kind=kCustom, calls=%fused_computation | custom fusion | bytes 50356224 | tf_op jit(solution)/shard_map/jit(_take)/gather | solution.py:157
  331.4 21.4 %select_select_fusion = bf16[4,1536,2048]{2,1,0:T(8,128)(2,1)} fusion(bf16[4,1536,2048]{2,1,0:T(8,128)(2,1)} %bitcast.28, pred[4,1536]{1,0:T(4,128)(4,1)S(1)} %get-tuple-element.17, pred[4,1536]{1,0:T(4,128)(4,1)S(1)} %get-tuple-element.19), kind=kLoop, calls=%fused_computation.1 | loop fusion | flops 25165824 | bytes 50343936 | tf_op jit(solution)/shard_map/jit(_where)/select_n | solution.py:158
  352.8 0.0 copy-start.10
  352.8 0.0 copy-start.11
  352.8 0.1 reduce-scatter.2.cloned.1.call-update
  352.9 0.1 all-gather.9.cloned.1.call-start
  353.0 0.5 copy-done.8
  353.5 0.0 copy-done.9
  353.5 0.0 copy-done.10
  353.5 0.0 copy-done.11
  353.5 133.1 %reduce-scatter.2.cloned.1.call-done = bf16[4,192,2048]{2,1,0:T(8,128)(2,1)} async-done(((bf16[4,1536,2048]{2,1,0:T(8,128)(2,1)}), bf16[4,192,2048]{2,1,0:T(8,128)(2,1)}) %reduce-scatter.2.cloned.1.call-update) | async-done | bytes 3145744 | tf_op jit(solution)/shard_map/reduce_scatter | solution.py:161
  486.6 2.5 convert_reduce_fusion.1
  489.1 2.9 fusion.8
  492.0 0.0 copy-done.4
  492.0 1.7 convert_reduce_fusion.2
  493.8 0.0 copy-start.2
  493.8 1.0 multiply_reduce_fusion
  494.8 0.7 copy-done.2
  495.5 2.9 add_convert_fusion.1
  498.3 0.1 all-gather.9.cloned.1.call-update
  498.4 0.2 all-gather.11.cloned.1.call-start
  498.7 118.1 %all-gather.9.cloned.1.call-done = bf16[4,1536,2048]{2,1,0:T(8,128)(2,1)} async-done(((bf16[4,192,2048]{2,1,0:T(8,128)(2,1)}), bf16[4,1536,2048]{2,1,0:T(8,128)(2,1)}) %all-gather.9.cloned.1.call-update) | async-done | bytes 25165840 | tf_op jit(solution)/shard_map/all_gather | solution.py:164
  616.8 2.4 constant_dynamic-slice_fusion
  619.2 0.1 all-gather.11.cloned.1.call-update
  619.2 0.0 copy-done.7
  619.2 0.6 broadcast_in_dim.54.pad_ref
  619.9 8.6 copy.28
  628.5 0.0 copy-done.16
  628.5 0.0 copy-done.17
  628.5 0.7 dynamic_slice.14.slope_ref
  629.2 26.6 %add_convert_fusion.q_ref.k_ref.v_ref = bf16[4,1536,768]{2,1,0:T(8,128)(2,1)} fusion(bf16[4,1536,2048]{2,1,0:T(8,128)(2,1)} %all-gather.9.cloned.1.call-done, bf16[2048,768,1]{0,1,2:T(8,128)(2,1)} %bitcast.32, f32[768]{0:T(1024)S(1)} %reshape.94), kind=kOutput, calls=%fused_computation.2 | convolution fusion | flops 19336790016 | bytes 37751808 | tf_op jit(solution)/shard_map/bsd,de->bse/dot_general | solution.py:166
  655.8 35.4 %attention.1 = bf16[4,1536,256]{2,1,0:T(8,128)(2,1)} custom-call(f32[2]{0:T(128)} %dynamic_slice.14.slope_ref, s32[4,1,1536]{2,1,0:T(1,128)} %broadcast_in_dim.54.pad_ref, bf16[4,1536,768]{2,1,0:T(8,128)(2,1)} %add_convert_fusion.q_ref.k_ref.v_ref, bf16[4,1536,768]{2,1,0:T(8,128)(2,1)} %add_convert_fusion.q_ref.k_ref.v_ref, ...), custom_call_target="tpu_custom_call" | custom-call | flops 9663676416 | bytes 14155776 | tf_op jit(solution)/shard_map/attention/pallas_call | solution.py:57
  691.1 0.0 copy-start.14
  691.1 0.0 copy-start.15
  691.1 4.0 copy.31
  695.1 4.7 all-to-all-start
  699.9 0.0 copy-done.12
  699.9 0.0 copy-done.13
  699.9 0.0 copy-done.15
  699.9 0.6 broadcast_in_dim.55.shift_ref
  700.5 8.4 copy.33
  708.9 54.4 %all-to-all-done = bf16[4,8,192,256]{3,2,0,1:T(8,128)(2,1)} async-done(((bf16[4,8,192,256]{3,2,0,1:T(8,128)(2,1)}), bf16[4,8,192,256]{3,2,0,1:T(8,128)(2,1)}, u32[]{:S(2)}, u32[]{:S(2)}) %all-to-all-start) | async-done | bytes 3145760 | tf_op jit(solution)/shard_map/all_to_all | solution.py:168
  763.3 3.8 copy.32
  767.1 1.1 copy.36
  768.2 0.3 copy-done.6
  768.6 7.2 convert_reduce_fusion
  775.8 1.0 fusion.4
  776.8 0.7 copy-done.5
  777.5 2.9 fusion.7.normed_ref
  780.3 35.9 %mlp_up.1.act_ref = bf16[768,8192]{1,0:T(8,128)(2,1)} custom-call(bf16[768,2048]{1,0:T(8,128)(2,1)} %fusion.7.normed_ref, bf16[4,8,528,1024]{3,2,1,0:T(8,128)(2,1)} %bitcast.35), custom_call_target="tpu_custom_call" | custom-call | flops 25769803776 | bytes 34603008 | tf_op jit(solution)/shard_map/mlp_up/pallas_call | solution.py:82
  816.2 41.1 %mlp_down.1 = bf16[768,2048]{1,0:T(8,128)(2,1)} custom-call(bf16[768,8192]{1,0:T(8,128)(2,1)} %mlp_up.1.act_ref, bf16[4,8,256,2048]{3,2,1,0:T(8,128)(2,1)} %bitcast.36, bf16[768,2048]{1,0:T(8,128)(2,1)} %copy-done.5, bf16[1,2048]{1,0:T(2,128)(2,1)} %broadcast_in_dim.55.shift_ref), custom_call_target="tpu_custom_call" | custom-call | flops 25769803776 | bytes 33554432 | tf_op jit(solution)/shard_map/mlp_down/pallas_call | solution.py:118
  857.4 0.0 copy-done.1
  (34 shorter events, 0.1 us)
Async XLA Ops:
  6.5 1.2 copy-start
  6.6 346.2 %all-gather.7.cloned.1.call-start = ((), (), s32[]{:S(2)}) async-start(), calls=%async_computation.3 | async-start | bytes 8650752 | tf_op jit(solution)/shard_map/all_gather | solution.py:144
  8.6 344.2 %all-gather.5.cloned.1.call-start = ((), (), s32[]{:S(2)}) async-start(), calls=%async_computation.2 | async-start | bytes 35684352 | tf_op jit(solution)/shard_map/all_gather | solution.py:144
  11.8 474.8 %reduce-scatter.2.cloned.1.call-start = ((), (), s32[]{:S(2)}) async-start(), calls=%async_computation.4 | async-start | bytes 28311552 | tf_op jit(solution)/shard_map/reduce_scatter | solution.py:161
  352.8 0.7 copy-start.8
  352.8 0.7 copy-start.9
  352.8 0.7 copy-start.10
  352.8 0.7 copy-start.11
  352.9 263.9 %all-gather.9.cloned.1.call-start = ((), (), s32[]{:S(2)}) async-start(), calls=%async_computation.5 | async-start | bytes 28311552 | tf_op jit(solution)/shard_map/all_gather | solution.py:164
  486.6 5.4 copy-start.4
  493.8 1.7 copy-start.2
  495.5 123.8 %copy-start.7 = (s32[4,1536]{1,0:T(4,128)S(1)}, s32[4,1536]{1,0:T(4,128)}, u32[]{:S(2)}) copy-start(s32[4,1536]{1,0:T(4,128)} %param.19) | copy-start | bytes 73732
  498.3 130.2 %copy-start.16 = (bf16[2,3,128]{2,0,1:T(2,128)(2,1)S(1)}, bf16[2,3,128]{2,0,1:T(2,128)(2,1)}, u32[]{:S(2)}) copy-start(bf16[2,3,128]{2,0,1:T(2,128)(2,1)} %param.26) | copy-start | bytes 4612
  498.3 130.2 %copy-start.17 = (f32[16]{0:T(128)S(1)}, f32[16]{0:T(128)}, u32[]{:S(2)}) copy-start(f32[16]{0:T(128)} %constant.62.clone) | copy-start | bytes 196
  498.4 317.8 %all-gather.11.cloned.1.call-start = ((), (), s32[]{:S(2)}) async-start(), calls=%async_computation.6 | async-start | bytes 34603008 | tf_op jit(solution)/shard_map/all_gather | solution.py:144
  691.1 8.7 %copy-start.12 = (bf16[2048]{0:T(1024)(128)(2,1)S(1)}, bf16[2048]{0:T(1024)(128)(2,1)}, u32[]{:S(2)}) copy-start(bf16[2048]{0:T(1024)(128)(2,1)} %param.28) | copy-start | bytes 12292
  691.1 8.8 %copy-start.13 = (bf16[2048]{0:T(1024)(128)(2,1)S(1)}, bf16[2048]{0:T(1024)(128)(2,1)}, u32[]{:S(2)}) copy-start(bf16[2048]{0:T(1024)(128)(2,1)} %param.30) | copy-start | bytes 12292
  691.1 8.8 %copy-start.14 = (bf16[2048]{0:T(1024)(128)(2,1)S(1)}, bf16[2048]{0:T(1024)(128)(2,1)}, u32[]{:S(2)}) copy-start(bf16[2048]{0:T(1024)(128)(2,1)} %param.29) | copy-start | bytes 12292
  691.1 8.8 %copy-start.15 = (bf16[2048]{0:T(1024)(128)(2,1)S(1)}, bf16[2048]{0:T(1024)(128)(2,1)}, u32[]{:S(2)}) copy-start(bf16[2048]{0:T(1024)(128)(2,1)} %param.34) | copy-start | bytes 12292
  695.1 68.2 %all-to-all-start = ((bf16[4,8,192,256]{3,2,0,1:T(8,128)(2,1)}), bf16[4,8,192,256]{3,2,0,1:T(8,128)(2,1)}, u32[]{:S(2)}, u32[]{:S(2)}) async-start(bf16[4,8,192,256]{3,2,0,1:T(8,128)(2,1)} %copy.31), calls=%async_computation.1 | async-start | bytes 6291456 | tf_op jit(solution)/shard_map/all_to_all | solution.py:168
  763.3 5.0 copy-start.3
  763.3 5.3 copy-start.6
  775.8 1.6 copy-start.5
  816.2 41.1 %copy-start.1 = (bf16[256,2048]{1,0:T(8,128)(2,1)S(1)}, bf16[256,2048]{1,0:T(8,128)(2,1)}, u32[]{:S(2)}) copy-start(bf16[256,2048]{1,0:T(8,128)(2,1)} %param.27) | copy-start | bytes 3145732
Sparse Core Ops, SparseCore 0:
  10.4 78.9 all-gather.6
  92.6 170.1 all-gather.4
  353.0 133.5 reduce-scatter.1
  498.5 118.2 all-gather.8
  619.6 167.5 all-gather.10
